TPU v7x, 128 devices: a whole 4x4x4 slice. The times are simulated.
128 devices in a mesh: inst: 2 (over core), pipe: 8 (over x_lo, z), tensor: 8 (over x_hi, y).
Axes of the slice: x: 4 (x_hi: 2, x_lo: 2; x = x_hi * 2 + x_lo), y: 4, z: 4, core: 2. Of those that a mesh axis runs over, the one named last changes fastest.
Arguments:
- lengths: int32 [2, 64], replicated, may hold values from 2 to 384, as said below
- page_table: int32 [2, 64, 3], P('inst'), may hold values from 0 to 191, as said below
- migration: int32 [16, 3], replicated, may hold values from 0 to 63, as said below
- dest_slots: int32 [16, 3], replicated, may hold values from 0 to 47, as said below
- queries: bfloat16 [2, 8, 64, 8192], P('inst', 'pipe', None, 'tensor'), may hold values from -64 to 64
- key_cache: bfloat16 [2, 8, 8, 24576, 128], P('inst', 'pipe', 'tensor'), may hold values from -64 to 64
- value_cache: bfloat16 [2, 8, 8, 24576, 128], P('inst', 'pipe', 'tensor'), may hold values from -5 to 5
- out_weight: bfloat16 [8, 8192, 8192], P('pipe', 'tensor'), may hold values from -0.09375 to 0.09375
Outputs:
- update: bfloat16 [2, 64, 8192], P('inst', None, ('pipe', 'tensor'))
- received_keys: bfloat16 [2, 8, 8, 6144, 128], P('inst', 'pipe', 'tensor')
- received_values: bfloat16 [2, 8, 8, 6144, 128], P('inst', 'pipe', 'tensor')
Inputs may be any that keep to these rules, and one draw needn't show every extreme that they name: `lengths`: in instance 1 every request holds more than 192 tokens and one holds exactly 384; in instance 0 every request holds at most 192. `page_table`: for each instance a permutation of its 192 pool pages, 3 for each request. `migration`: rows 0 to 7 name source instance 1 and destination instance 0, the other rows source 0 and destination 1; the requests of all rows are distinct numbers, and the one in row 0 holds at most (2) * 128 tokens. `dest_slots`: A permutation of the 48 receive slots.
All inputs are finite; a program needn't handle non-finite values.
Results may differ from a plain program's by a relative error of at most 0.018.
Values may be sent and summed in bfloat16 or wider, within the bound.
No kernel may reach another device: no remote copies, remote signals or barrier semaphores. Data moves between devices by JAX's collectives and lax.ppermute only.
A program may use at most 128 MiB of HBM per device.

v0:
```python
import math

import jax
import jax.numpy as jnp
from jax import lax
from jax.sharding import PartitionSpec as P

PAGE = 128


def from_partner(array, axis, stride):
    return lax.ppermute(array, axis, [(i, i ^ 1 << stride) for i in range(lax.axis_size(axis))])


def cut_along(array, dim, devices):
    before, after = (array.shape[:dim], array.shape[dim + 1 :])
    return jnp.moveaxis(array.reshape(*before, devices, -1, *after), dim, 0)


def summed_on_arrival(array, axis, dim):
    pieces = cut_along(array, dim, lax.axis_size(axis))
    arrived = lax.all_to_all(pieces, axis, split_axis=0, concat_axis=0, tiled=True)
    return arrived.astype(jnp.float32).sum(axis=0)


def attend(query_block, key_pages, value_pages, page_map, length_list, page_bound):
    row_count, kv_heads, group_size, head_dim = query_block.shape
    page_size = key_pages.shape[2]
    scale_factor = 1.0 / math.sqrt(head_dim)
    offsets = jnp.arange(page_size, dtype=jnp.int32)

    def advance(page_index, carry):
        running_max, running_sum, accumulated = carry
        slot_ids = lax.dynamic_index_in_dim(page_map, page_index, 1, keepdims=False)
        key_block = key_pages[:, slot_ids]
        value_block = value_pages[:, slot_ids]
        scores = (
            jnp.einsum(
                "rkgd,krtd->rkgt", query_block, key_block, preferred_element_type=jnp.float32
            )
            * scale_factor
        )
        visible = ((page_index * page_size + offsets)[None, :] < length_list[:, None])[
            :, None, None, :
        ]
        scores = jnp.where(visible, scores, -1e30)
        new_max = jnp.maximum(running_max, jnp.max(scores, axis=-1))
        fading = jnp.exp(running_max - new_max)
        weights = jnp.where(visible, jnp.exp(scores - new_max[..., None]), 0.0)
        running_sum = running_sum * fading + jnp.sum(weights, axis=-1)
        accumulated = accumulated * fading[..., None] + jnp.einsum(
            "rkgt,krtd->rkgd", weights, value_block.astype(jnp.float32)
        )
        return (new_max, running_sum, accumulated)

    initial = (
        jnp.full((row_count, kv_heads, group_size), -1e30, jnp.float32),
        jnp.zeros((row_count, kv_heads, group_size), jnp.float32),
        jnp.zeros((row_count, kv_heads, group_size, head_dim), jnp.float32),
    )
    running_max, running_sum, accumulated = lax.fori_loop(0, page_bound, advance, initial)
    return (
        (accumulated / running_sum[..., None])
        .reshape(row_count, kv_heads * group_size * head_dim)
        .astype(jnp.bfloat16)
    )


def body(lengths, page_table, migration, dest_slots, queries, key_cache, value_cache, out_weight):
    kv_heads = key_cache.shape[2]
    head_dim = key_cache.shape[4]
    row_count = page_table.shape[1]
    max_pages = page_table.shape[2]
    pool_pages = key_cache.shape[3] // PAGE
    group_size = queries.shape[3] // head_dim // kv_heads
    myself = lax.axis_index("inst")
    movers = migration[:, 0]
    sources = migration[:, 1]
    outgoing_rows = sources == myself
    own_lengths = lax.dynamic_index_in_dim(lengths, myself, 0, keepdims=False)
    moved_lengths = lengths[sources, movers]
    page_map = page_table[0]
    key_pages = key_cache[0, 0].reshape(kv_heads, pool_pages, PAGE, head_dim)
    value_pages = value_cache[0, 0].reshape(kv_heads, pool_pages, PAGE, head_dim)
    live_pages = (
        (jnp.arange(max_pages, dtype=jnp.int32)[None, :] * PAGE < moved_lengths[:, None])
        & outgoing_rows[:, None]
    ).reshape(-1)
    out_slots = page_map[movers].reshape(-1)
    outgoing_keys = jnp.where(
        live_pages[None, :, None, None], key_pages[:, out_slots], jnp.zeros((), key_cache.dtype)
    )
    outgoing_values = jnp.where(
        live_pages[None, :, None, None], value_pages[:, out_slots], jnp.zeros((), value_cache.dtype)
    )
    query_block = queries[0, 0].reshape(row_count, kv_heads, group_size, head_dim)
    got_keys, got_values = from_partner((outgoing_keys, outgoing_values), "inst", 0)
    local_bound = (jnp.max(own_lengths) + PAGE - 1) // PAGE
    attended = attend(query_block, key_pages, value_pages, page_map, own_lengths, local_bound)
    recv_slots = dest_slots.reshape(-1)
    recv_count = recv_slots.shape[0]
    received_keys = (
        jnp.zeros((kv_heads, recv_count, PAGE, head_dim), key_cache.dtype)
        .at[:, recv_slots]
        .set(got_keys)
    )
    received_values = (
        jnp.zeros((kv_heads, recv_count, PAGE, head_dim), value_cache.dtype)
        .at[:, recv_slots]
        .set(got_values)
    )
    layer_term = jnp.dot(attended, out_weight[0], preferred_element_type=jnp.float32)
    partial_total = summed_on_arrival(layer_term.astype(jnp.bfloat16), "pipe", 1)
    summed = summed_on_arrival(partial_total.astype(jnp.bfloat16), "tensor", 1)
    update = summed.astype(jnp.bfloat16)[None]
    received_keys = received_keys.reshape(1, 1, kv_heads, recv_count * PAGE, head_dim)
    received_values = received_values.reshape(1, 1, kv_heads, recv_count * PAGE, head_dim)
    return (update, received_keys, received_values)


def solution(mesh):
    placed = (
        P(),
        P("inst", None, None),
        P(),
        P(),
        P("inst", "pipe", None, "tensor"),
        P("inst", "pipe", "tensor", None, None),
        P("inst", "pipe", "tensor", None, None),
        P("pipe", "tensor", None),
    )
    return jax.shard_map(
        body,
        mesh=mesh,
        in_specs=placed,
        out_specs=(
            P("inst", None, ("pipe", "tensor")),
            P("inst", "pipe", "tensor", None, None),
            P("inst", "pipe", "tensor", None, None),
        ),
        check_vma=False,
    )
```

profile of v0, /device:TPU:1, one launch (start us, length us, event | category | flops | bytes accessed | tf_op | source)
XLA Modules:
  0.0 99.6 jit_solution(17108989888161859060)
XLA Ops:
  2.9 1.4 %gather_fusion.2 = s32[16]{0:T(128)S(1)} fusion(s32[2,64]{1,0:T(2,128)} %param.10, s32[16]{0:T(128)S(1)} %get-tuple-element.151), kind=kCustom, calls=%fused_computation.2 | custom fusion | bytes 256 | tf_op jit(solution)/shard_map/gather | solution.py:81
  5.1 3.6 %gather_fusion.4 = bf16[48,128,128]{2,1,0:T(8,128)(2,1)S(1)} fusion(bf16[192,128,128]{2,1,0:T(8,128)(2,1)} %bitcast.100, s32[1024]{0:T(1024)S(1)} %pad_clamp_fusion.1), kind=kCustom, calls=%fused_computation.4 | custom fusion | bytes 3145920 | tf_op jit(solution)/shard_map/gather | solution.py:91
  8.8 3.6 %gather_fusion.5 = bf16[48,128,128]{2,1,0:T(8,128)(2,1)S(1)} fusion(bf16[192,128,128]{2,1,0:T(8,128)(2,1)} %bitcast.103, s32[1024]{0:T(1024)S(1)} %pad_clamp_fusion.1), kind=kCustom, calls=%fused_computation.5 | custom fusion | bytes 3145920 | tf_op jit(solution)/shard_map/gather | solution.py:94
  12.4 1.9 %bitcast_select_fusion = (bf16[1,48,128,128]{3,2,1,0:T(8,128)(2,1)}, bf16[1,48,128,128]{3,2,1,0:T(8,128)(2,1)}) fusion(bf16[48,128,128]{2,1,0:T(8,128)(2,1)S(1)} %gather_fusion.5, pred[48]{0:T(512)(128)(4,1)S(1)} %and.27, bf16[48,128,128]{2,1,0:T(8,128)(2,1)S(1)} %gather_fusion.4), kind=kLoop, calls=%fused_computation.33 | loop fusion | flops 1572864 | bytes 6291504 | tf_op jit(solution)/shard_map/jit(_where)/select_n | solution.py:93
  14.4 1.4 %collective-permute-start = (bf16[1,48,128,128]{3,2,1,0:T(8,128)(2,1)}, bf16[1,48,128,128]{3,2,1,0:T(8,128)(2,1)}, u32[]{:S(2)}, u32[]{:S(2)}) collective-permute-start(bf16[1,48,128,128]{3,2,1,0:T(8,128)(2,1)} %get-tuple-element.156), channel_id=1, source_target_pairs={{0,64},{64,0},{1,65},{65,1},{2,66},{66,2},{3,67},{67,3},{4,68},{68... | collective-permute-start | bytes 4718600 | tf_op jit(solution)/shard_map/ppermute | solution.py:12
  17.2 29.8 %while.15 = (s32[]{:T(128)}, f32[64,1,8]{2,0,1:T(8,128)S(1)}, f32[64,1,8]{2,0,1:T(8,128)S(1)}, f32[64,1,8,128]{3,2,0,1:T(8,128)S(1)}, s32[]{:T(128)}, /*index=5*...) while((s32[]{:T(128)}, f32[64,1,8]{2,0,1:T(8,128)S(1)}, ...), condition=%wide.region_4.5_spmd.clone, body=%wide.region_1.4_spmd.clone.sunk | while | flops 34220868 | bytes 14097083 | solution.py:61
  17.3 3.7 %gather_fusion = bf16[64,128,128]{2,1,0:T(8,128)(2,1)S(1)} fusion(bf16[192,128,128]{2,1,0:T(8,128)(2,1)} %bitcast.102, s32[1024]{0:T(1024)S(1)} %pad_clamp_fusion.4), kind=kCustom, calls=%fused_computation.clone.clone.1 | custom fusion | bytes 4194560 | tf_op jit(solution)/shard_map/while/body/gather | solution.py:35
  21.1 1.3 %fusion.42 = (f32[64,8]{1,0:T(8,128)S(1)}, f32[64,8,128]{2,1,0:T(8,128)S(1)}) fusion(bf16[64,128,128]{2,1,0:T(8,128)(2,1)S(1)} %gather_fusion, bf16[64,1,8,128]{3,2,0,1:T(8,128)(2,1)S(1)} %get-tuple-element.263, pred[64,128]{1,0:T(8,128)(4,1)S(1)} %broadcast_compare_fusion.2), kind=kOutput, calls=%fused_computation.58.clone.1 | convolution fusion | flops 16973312 | bytes 2500608 | tf_op jit(solution)/shard_map/while/body/rkgd,krtd->rkgt/dot_general | solution.py:38
  22.4 3.7 %gather_fusion.1 = bf16[64,128,128]{2,1,0:T(8,128)(2,1)S(1)} fusion(bf16[192,128,128]{2,1,0:T(8,128)(2,1)} %bitcast.105, s32[1024]{0:T(1024)S(1)} %pad_clamp_fusion.4), kind=kCustom, calls=%fused_computation.1.clone.clone.1 | custom fusion | bytes 4194560 | tf_op jit(solution)/shard_map/while/body/gather | solution.py:36
  27.2 3.7 %gather_fusion = bf16[64,128,128]{2,1,0:T(8,128)(2,1)S(1)} fusion(bf16[192,128,128]{2,1,0:T(8,128)(2,1)} %bitcast.102, s32[1024]{0:T(1024)S(1)} %pad_clamp_fusion.4), kind=kCustom, calls=%fused_computation.clone.clone.1 | custom fusion | bytes 4194560 | tf_op jit(solution)/shard_map/while/body/gather | solution.py:35
  31.0 1.3 %fusion.42 = (f32[64,8]{1,0:T(8,128)S(1)}, f32[64,8,128]{2,1,0:T(8,128)S(1)}) fusion(bf16[64,128,128]{2,1,0:T(8,128)(2,1)S(1)} %gather_fusion, bf16[64,1,8,128]{3,2,0,1:T(8,128)(2,1)S(1)} %get-tuple-element.263, pred[64,128]{1,0:T(8,128)(4,1)S(1)} %broadcast_compare_fusion.2), kind=kOutput, calls=%fused_computation.58.clone.1 | convolution fusion | flops 16973312 | bytes 2500608 | tf_op jit(solution)/shard_map/while/body/rkgd,krtd->rkgt/dot_general | solution.py:38
  32.3 3.7 %gather_fusion.1 = bf16[64,128,128]{2,1,0:T(8,128)(2,1)S(1)} fusion(bf16[192,128,128]{2,1,0:T(8,128)(2,1)} %bitcast.105, s32[1024]{0:T(1024)S(1)} %pad_clamp_fusion.4), kind=kCustom, calls=%fused_computation.1.clone.clone.1 | custom fusion | bytes 4194560 | tf_op jit(solution)/shard_map/while/body/gather | solution.py:36
  37.1 3.7 %gather_fusion = bf16[64,128,128]{2,1,0:T(8,128)(2,1)S(1)} fusion(bf16[192,128,128]{2,1,0:T(8,128)(2,1)} %bitcast.102, s32[1024]{0:T(1024)S(1)} %pad_clamp_fusion.4), kind=kCustom, calls=%fused_computation.clone.clone.1 | custom fusion | bytes 4194560 | tf_op jit(solution)/shard_map/while/body/gather | solution.py:35
  40.9 1.3 %fusion.42 = (f32[64,8]{1,0:T(8,128)S(1)}, f32[64,8,128]{2,1,0:T(8,128)S(1)}) fusion(bf16[64,128,128]{2,1,0:T(8,128)(2,1)S(1)} %gather_fusion, bf16[64,1,8,128]{3,2,0,1:T(8,128)(2,1)S(1)} %get-tuple-element.263, pred[64,128]{1,0:T(8,128)(4,1)S(1)} %broadcast_compare_fusion.2), kind=kOutput, calls=%fused_computation.58.clone.1 | convolution fusion | flops 16973312 | bytes 2500608 | tf_op jit(solution)/shard_map/while/body/rkgd,krtd->rkgt/dot_general | solution.py:38
  42.2 3.7 %gather_fusion.1 = bf16[64,128,128]{2,1,0:T(8,128)(2,1)S(1)} fusion(bf16[192,128,128]{2,1,0:T(8,128)(2,1)} %bitcast.105, s32[1024]{0:T(1024)S(1)} %pad_clamp_fusion.4), kind=kCustom, calls=%fused_computation.1.clone.clone.1 | custom fusion | bytes 4194560 | tf_op jit(solution)/shard_map/while/body/gather | solution.py:36
  47.1 8.8 %fusion.15 = bf16[64,8192]{1,0:T(8,128)(2,1)S(1)} fusion(bf16[1,1024,8192]{2,1,0:T(8,128)(2,1)} %param.17, bf16[8,8,8,128]{3,2,1,0:T(8,128)(2,1)S(1)} %bitcast.113), kind=kOutput, calls=%fused_computation.32 | convolution fusion | flops 1074266112 | bytes 17956864 | tf_op jit(solution)/shard_map/dot_general | solution.py:112
  55.9 1.1 %copy.35 = bf16[8,8,8,1024]{3,2,0,1:T(8,128)(2,1)} copy(bf16[8,8,8,1024]{3,2,1,0:T(8,128)(2,1)S(1)} %bitcast.111) | data formatting | bytes 2097152 | tf_op jit(solution)/shard_map/reshape | solution.py:17
  57.0 6.2 %all-to-all-start = ((bf16[8,64,1024]{2,1,0:T(8,128)(2,1)}), bf16[8,64,1024]{2,1,0:T(8,128)(2,1)S(1)}, u32[]{:S(2)}, u32[]{:S(2)}) async-start(bf16[8,64,1024]{2,1,0:T(8,128)(2,1)} %bitcast.79), calls=%async_computation | async-start | bytes 2097152 | tf_op jit(solution)/shard_map/all_to_all | solution.py:22
  63.4 9.3 %all-to-all-done = bf16[8,64,1024]{2,1,0:T(8,128)(2,1)S(1)} async-done(((bf16[8,64,1024]{2,1,0:T(8,128)(2,1)}), bf16[8,64,1024]{2,1,0:T(8,128)(2,1)S(1)}, u32[]{:S(2)}, u32[]{:S(2)}) %all-to-all-start) | async-done | bytes 1048608 | tf_op jit(solution)/shard_map/all_to_all | solution.py:22
  73.5 6.4 %all-to-all-start.1 = ((bf16[8,64,128]{2,1,0:T(8,128)(2,1)}), bf16[8,64,128]{2,1,0:T(8,128)(2,1)S(1)}, u32[]{:S(2)}, u32[]{:S(2)}) async-start(bf16[8,64,128]{2,1,0:T(8,128)(2,1)} %copy.24), calls=%async_computation.1 | async-start | bytes 262144 | tf_op jit(solution)/shard_map/all_to_all | solution.py:22
  79.9 6.9 %all-to-all-done.1 = bf16[8,64,128]{2,1,0:T(8,128)(2,1)S(1)} async-done(((bf16[8,64,128]{2,1,0:T(8,128)(2,1)}), bf16[8,64,128]{2,1,0:T(8,128)(2,1)S(1)}, u32[]{:S(2)}, u32[]{:S(2)}) %all-to-all-start.1) | async-done | bytes 131104 | tf_op jit(solution)/shard_map/all_to_all | solution.py:22
  87.8 5.1 %scatter_fusion = bf16[48,128,128]{2,1,0:T(8,128)(2,1)S(1)} fusion(bf16[48,128,128]{2,1,0:T(8,128)(2,1)S(1)} %broadcast.169.clone, s32[48]{0:T(128)S(1)} %fusion.20, bf16[48,128,128]{2,1,0:T(8,128)(2,1)} %bitcast.16), kind=kCustom, calls=%fused_computation.6 | custom fusion | bytes 4718784 | tf_op jit(solution)/shard_map/scatter | solution.py:105
  93.3 5.1 %scatter_fusion.1 = bf16[48,128,128]{2,1,0:T(8,128)(2,1)S(1)} fusion(bf16[48,128,128]{2,1,0:T(8,128)(2,1)S(1)} %broadcast.169.clone.1, s32[48]{0:T(128)S(1)} %fusion.20, bf16[48,128,128]{2,1,0:T(8,128)(2,1)} %bitcast.20), kind=kCustom, calls=%fused_computation.7 | custom fusion | bytes 4718784 | tf_op jit(solution)/shard_map/scatter | solution.py:110
  98.4 1.1 %copy-done.1 = bf16[48,128,128]{2,1,0:T(8,128)(2,1)} copy-done((bf16[48,128,128]{2,1,0:T(8,128)(2,1)}, bf16[48,128,128]{2,1,0:T(8,128)(2,1)S(1)}, u32[]{:S(2)}) %copy-start.1) | copy-done | bytes 1572888
  (66 shorter events, 9.6 us)
Async XLA Ops:
  12.4 3.4 %copy-start = (s32[2,64]{1,0:T(2,128)S(1)}, s32[2,64]{1,0:T(2,128)}, u32[]{:S(2)}) copy-start(s32[2,64]{1,0:T(2,128)} %param.10) | copy-start | bytes 1540
  12.4 4.7 %copy-start.3 = (bf16[1,1,64,1024]{3,2,1,0:T(8,128)(2,1)S(1)}, bf16[1,1,64,1024]{3,2,1,0:T(8,128)(2,1)}, u32[]{:S(2)}) copy-start(bf16[1,1,64,1024]{3,2,1,0:T(8,128)(2,1)} %param.14) | copy-start | bytes 393220
  14.4 73.1 %collective-permute-start = (bf16[1,48,128,128]{3,2,1,0:T(8,128)(2,1)}, bf16[1,48,128,128]{3,2,1,0:T(8,128)(2,1)}, u32[]{:S(2)}, u32[]{:S(2)}) collective-permute-start(bf16[1,48,128,128]{3,2,1,0:T(8,128)(2,1)} %get-tuple-element.156), channel_id=1, source_target_pairs={{0,64},{64,0},{1,65},{65,1},{2,66},{66,2},{3,67},{67,3},{4,68},{68... | collective-permute-start | bytes 4718600 | tf_op jit(solution)/shard_map/ppermute | solution.py:12
  15.7 77.2 %collective-permute-start.1 = (bf16[1,48,128,128]{3,2,1,0:T(8,128)(2,1)}, bf16[1,48,128,128]{3,2,1,0:T(8,128)(2,1)}, u32[]{:S(2)}, u32[]{:S(2)}) collective-permute-start(bf16[1,48,128,128]{3,2,1,0:T(8,128)(2,1)} %get-tuple-element.155), channel_id=1, source_target_pairs={{0,64},{64,0},{1,65},{65,1},{2,66},{66,2},{3,67},{67,3},{4,68},{68... | collective-permute-start | bytes 4718600 | tf_op jit(solution)/shard_map/ppermute | solution.py:12
  57.0 6.2 %copy-start.4 = (s32[16,3]{0,1:T(4,128)S(1)}, s32[16,3]{0,1:T(4,128)}, u32[]{:S(2)}) copy-start(s32[16,3]{0,1:T(4,128)} %param.13) | copy-start | bytes 580
  57.0 15.7 %all-to-all-start = ((bf16[8,64,1024]{2,1,0:T(8,128)(2,1)}), bf16[8,64,1024]{2,1,0:T(8,128)(2,1)S(1)}, u32[]{:S(2)}, u32[]{:S(2)}) async-start(bf16[8,64,1024]{2,1,0:T(8,128)(2,1)} %bitcast.79), calls=%async_computation | async-start | bytes 2097152 | tf_op jit(solution)/shard_map/all_to_all | solution.py:22
  73.5 13.3 %all-to-all-start.1 = ((bf16[8,64,128]{2,1,0:T(8,128)(2,1)}), bf16[8,64,128]{2,1,0:T(8,128)(2,1)S(1)}, u32[]{:S(2)}, u32[]{:S(2)}) async-start(bf16[8,64,128]{2,1,0:T(8,128)(2,1)} %copy.24), calls=%async_computation.1 | async-start | bytes 262144 | tf_op jit(solution)/shard_map/all_to_all | solution.py:22
  92.9 5.5 %copy-start.2 = (bf16[48,128,128]{2,1,0:T(8,128)(2,1)}, bf16[48,128,128]{2,1,0:T(8,128)(2,1)S(1)}, u32[]{:S(2)}) copy-start(bf16[48,128,128]{2,1,0:T(8,128)(2,1)S(1)} %scatter_fusion) | copy-start | bytes 4718596
  98.4 1.1 %copy-start.1 = (bf16[48,128,128]{2,1,0:T(8,128)(2,1)}, bf16[48,128,128]{2,1,0:T(8,128)(2,1)S(1)}, u32[]{:S(2)}) copy-start(bf16[48,128,128]{2,1,0:T(8,128)(2,1)S(1)} %scatter_fusion.1) | copy-start | bytes 4718596
where the time goes:
time: 100 us; the launch traced here: 99.6 us
  local copies, waits for them, and re-layouts  46.7 us (47%)
  waiting for transfers between devices  16.2 us (16%)
  matrix products  14.7 us (15%)
  starting transfers between devices  13.9 us (14%)
  other arithmetic  6.19 us (6%)
  between operations  1.53 us (2%)
    all_to_all x2, waiting for transfers between devices, summed_on_arrival(): lax.all_to_all(pieces, axis, split_axis=0, concat_axis=0, tiled=True)  16.2 us
    all_to_all x2, starting transfers between devices, summed_on_arrival(): lax.all_to_all(pieces, axis, split_axis=0, concat_axis=0, tiled=True)  12.6 us
    gather x3, local copies, waits for them, and re-layouts, advance(): value_block = value_pages[:, slot_ids]  11.2 us
    gather x3, local copies, waits for them, and re-layouts, advance(): key_block = key_pages[:, slot_ids]  11.2 us
    dot_general x1, matrix products, body(): jnp.dot(attended, out_weight[0], preferred_element_type=jnp.float32)  8.79 us
    scatter x1, local copies, waits for them, and re-layouts, body(): received_keys = jnp.zeros((kv_heads, recv_count, PAGE, head_dim), key_cac...  5.1 us
    scatter x1, local copies, waits for them, and re-layouts, body(): received_values = jnp.zeros((kv_heads, recv_count, PAGE, head_dim), value...  5.1 us
    dot_general x3, matrix products, advance(): jnp.einsum('rkgd,krtd->rkgt', query_block, key_block, preferred_element_t...  3.8 us
  transfers between devices with their start and end apart: 4, of which 2 were waited for; matrix products, arithmetic and copies ran while one was open for 48% of the time, Pallas kernels for 0%

commit v1 on v0

v1 whole, which is shorter than its diff:
```python
import functools
import math

import jax
import jax.numpy as jnp
from jax import lax
from jax.experimental import pallas as pl
from jax.experimental.pallas import tpu as pltpu
from jax.sharding import PartitionSpec as P


PAGE = 128
GROUP = 8
CHUNK = 512

ANY = pl.BlockSpec(memory_space=pltpu.HBM)
SMEM = pl.BlockSpec(memory_space=pltpu.SMEM)
VMEM = pl.BlockSpec(memory_space=pltpu.VMEM)


def attend_kernel(
    rows, heads, pages,
    lengths, page_table, queries, keys, values, weight,
    out,
    q32, kbuf, vbuf, wbuf, attended, ksem, vsem, wsem,
):
    inst = lax.axis_index("inst")
    head_dim = keys.shape[1]
    blocks = rows // GROUP
    chunks = wbuf.shape[0]
    span = pages * PAGE
    scale = 1.0 / math.sqrt(head_dim)

    def fetch_pages(block):
        for g in range(GROUP):
            for p in range(pages):
                start = pl.multiple_of(page_table[p, 0, block * GROUP + g] * PAGE, PAGE)
                at = pl.ds((g * pages + p) * PAGE, PAGE)
                source = pl.ds(start, PAGE)
                pltpu.make_async_copy(keys.at[source], kbuf.at[block, at], ksem.at[block]).start()
                pltpu.make_async_copy(values.at[source], vbuf.at[block, at], vsem.at[block]).start()

    def weight_copy(chunk):
        at = pl.ds(pl.multiple_of(chunk * CHUNK, CHUNK), CHUNK)
        return pltpu.make_async_copy(weight.at[:, at], wbuf.at[chunk], wsem.at[chunk])

    fetch_pages(0)
    fetch_pages(1)
    q32[...] = queries[...].astype(jnp.float32)
    row_in_group = lax.broadcasted_iota(jnp.int32, (heads * GROUP, 1), 0) % GROUP
    token = lax.broadcasted_iota(jnp.int32, (heads * GROUP, span), 1)

    def attend_block(block, _):
        @pl.when(block + 2 < blocks)
        def _():
            fetch_pages(block + 2)

        for j in range(chunks // blocks):
            weight_copy(block * (chunks // blocks) + j).start()
        first = pl.multiple_of(block * GROUP, GROUP)
        q = q32[pl.ds(first, GROUP), :]
        q = jnp.concatenate(
            [q[:, h * head_dim : (h + 1) * head_dim] for h in range(heads)], axis=0
        ).astype(jnp.bfloat16)
        whole = pl.ds(0, GROUP * span)
        pltpu.make_async_copy(keys.at[whole], kbuf.at[block], ksem.at[block]).wait()
        scores = jnp.zeros((heads * GROUP, span), jnp.float32)
        limit = jnp.zeros((heads * GROUP, 1), jnp.int32)
        for g in range(GROUP):
            k = kbuf[block, g * span : (g + 1) * span, :]
            one = lax.dot_general(
                q, k, (((1,), (1,)), ((), ())), preferred_element_type=jnp.float32
            )
            mine = row_in_group == g
            scores = jnp.where(mine, one, scores)
            limit = jnp.where(mine, lengths[inst, block * GROUP + g], limit)
        scores = jnp.where(token < limit, scores, -1e30)
        top = jnp.max(scores, axis=1, keepdims=True)
        weights = jnp.exp((scores - top) * scale)
        total = jnp.sum(weights, axis=1, keepdims=True)
        weights = weights.astype(jnp.bfloat16)
        pltpu.make_async_copy(values.at[whole], vbuf.at[block], vsem.at[block]).wait()
        result = jnp.zeros((heads * GROUP, head_dim), jnp.float32)
        for g in range(GROUP):
            v = vbuf[block, g * span : (g + 1) * span, :]
            one = jnp.dot(weights, v, preferred_element_type=jnp.float32)
            result = jnp.where(row_in_group == g, one, result)
        result = result / total
        for h in range(heads):
            attended[pl.ds(first, GROUP), h * head_dim : (h + 1) * head_dim] = result[
                h * GROUP : (h + 1) * GROUP, :
            ]
        return 0

    lax.fori_loop(0, blocks, attend_block, 0)
    rounded = attended[...].astype(jnp.bfloat16)

    def project(chunk, _):
        weight_copy(chunk).wait()
        part = jnp.dot(rounded, wbuf[chunk], preferred_element_type=jnp.float32)
        width = out.shape[2]
        for j in range(CHUNK // width):
            out[chunk * (CHUNK // width) + j] = part[:, j * width : (j + 1) * width].astype(
                out.dtype
            )
        return 0

    lax.fori_loop(0, chunks, project, 0)


def attend_project(lengths, page_table, queries, keys, values, weight, parts):
    rows, width = queries.shape
    head_dim = keys.shape[1]
    heads = width // head_dim
    pages = page_table.shape[0]
    blocks = rows // GROUP
    depth, columns = weight.shape
    chunks = columns // CHUNK
    return pl.pallas_call(
        functools.partial(attend_kernel, rows, heads, pages),
        out_shape=jax.ShapeDtypeStruct((parts, rows, columns // parts), jnp.bfloat16),
        in_specs=[SMEM, SMEM, VMEM, ANY, ANY, ANY],
        out_specs=VMEM,
        scratch_shapes=[
            pltpu.VMEM((rows, width), jnp.float32),
            pltpu.VMEM((blocks, GROUP * pages * PAGE, head_dim), keys.dtype),
            pltpu.VMEM((blocks, GROUP * pages * PAGE, head_dim), values.dtype),
            pltpu.VMEM((chunks, depth, CHUNK), weight.dtype),
            pltpu.VMEM((rows, width), jnp.float32),
            pltpu.SemaphoreType.DMA((blocks,)),
            pltpu.SemaphoreType.DMA((blocks,)),
            pltpu.SemaphoreType.DMA((chunks,)),
        ],
        compiler_params=pltpu.CompilerParams(vmem_limit_bytes=60 * 1024 * 1024),
        cost_estimate=pl.CostEstimate(
            flops=2 * rows * depth * columns + 4 * rows * width * pages * PAGE,
            bytes_accessed=2 * (weight.size + 2 * keys.size),
            transcendentals=0,
        ),
        name="attend_project",
    )(lengths, page_table, queries, keys, values, weight)


def outgoing_kernel(moves, pages, lengths, page_table, migration, dest_slots, after, keys, values,
                    key_image, value_image, ksem, vsem):
    inst = lax.axis_index("inst")
    key_image[...] = jnp.zeros_like(key_image)
    value_image[...] = jnp.zeros_like(value_image)

    def each(act):
        for k in range(moves):
            move = (1 - inst) * moves + k
            request = migration[0, move]
            held = lengths[inst, request]
            for p in range(pages):
                source = pl.multiple_of(page_table[p, 0, request] * PAGE, PAGE)
                target = pl.multiple_of(dest_slots[p, move] * PAGE, PAGE)

                @pl.when(p * PAGE < held)
                def _():
                    for cache, image, sem in (
                        (keys, key_image, ksem), (values, value_image, vsem)
                    ):
                        act(
                            pltpu.make_async_copy(
                                cache.at[pl.ds(source, PAGE)],
                                image.at[pl.ds(target, PAGE)],
                                sem.at[k * pages + p],
                            )
                        )

    each(lambda copy: copy.start())
    each(lambda copy: copy.wait())


def outgoing(lengths, page_table, migration, dest_slots, after, keys, values):
    moves = migration.shape[1] // 2
    pages = page_table.shape[0]
    image = jax.ShapeDtypeStruct((dest_slots.size * PAGE, keys.shape[1]), keys.dtype)
    return pl.pallas_call(
        functools.partial(outgoing_kernel, moves, pages),
        out_shape=(image, image),
        in_specs=[SMEM, SMEM, SMEM, SMEM, ANY, ANY, ANY],
        out_specs=(VMEM, VMEM),
        scratch_shapes=[
            pltpu.SemaphoreType.DMA((moves * pages,)),
            pltpu.SemaphoreType.DMA((moves * pages,)),
        ],
        compiler_params=pltpu.CompilerParams(vmem_limit_bytes=60 * 1024 * 1024),
        cost_estimate=pl.CostEstimate(
            flops=1_000_000, bytes_accessed=3 * 2 * image.size, transcendentals=0
        ),
        name="outgoing",
    )(lengths, page_table, migration, dest_slots, after, keys, values)


def body(lengths, page_table, migration, dest_slots, queries, key_cache, value_cache, out_weight):
    page_table = jnp.transpose(page_table, (2, 0, 1))
    migration, dest_slots = migration.T, dest_slots.T
    parts = lax.axis_size("pipe") * lax.axis_size("tensor")
    keys = key_cache.reshape(key_cache.shape[3:])
    values = value_cache.reshape(value_cache.shape[3:])
    partial = attend_project(
        lengths, page_table, queries.reshape(queries.shape[2:]), keys, values,
        out_weight.reshape(out_weight.shape[1:]), parts,
    )
    arrived = lax.all_to_all(partial, ("pipe", "tensor"), split_axis=0, concat_axis=0, tiled=True)
    images = outgoing(lengths, page_table, migration, dest_slots, partial, keys, values)
    received = [lax.ppermute(image, "inst", [(0, 1), (1, 0)]) for image in images]
    update = arrived.astype(jnp.float32).sum(axis=0).astype(jnp.bfloat16)
    return (update[None], *[r.reshape(1, 1, 1, *r.shape) for r in received])


def solution(mesh):
    placed = (
        P(),
        P("inst", None, None),
        P(),
        P(),
        P("inst", "pipe", None, "tensor"),
        P("inst", "pipe", "tensor", None, None),
        P("inst", "pipe", "tensor", None, None),
        P("pipe", "tensor", None),
    )
    return jax.shard_map(
        body,
        mesh=mesh,
        in_specs=placed,
        out_specs=(
            P("inst", None, ("pipe", "tensor")),
            P("inst", "pipe", "tensor", None, None),
            P("inst", "pipe", "tensor", None, None),
        ),
        check_vma=False,
    )
```

time: 100 us -> 56.2 us (0.56)
  the two profiles are of different devices: /device:TPU:1 before, /device:TPU:0 now
where the time goes in v1:
time: 56.2 us; the launch traced here: 55.9 us
  blocking collectives  29.4 us (52%)
  Pallas kernels  20.7 us (37%)
  local copies, waits for them, and re-layouts  3.8 us (7%)
  other arithmetic  0.78 us (1%)
  between operations  0.67 us (1%)
  starting transfers between devices  0.58 us (1%)
    all_to_all x1, blocking collectives, body(): lax.all_to_all(partial, ('pipe', 'tensor'), split_axis=0, concat_axis=0,...  29.4 us
    pallas_call x1, Pallas kernels, attend_project(): pl.pallas_call(functools.partial(attend_kernel, rows, heads, pages), out_...  16.2 us
    pallas_call x1, Pallas kernels, outgoing(): pl.pallas_call(functools.partial(outgoing_kernel, moves, pages), out_shap...  4.45 us
    unnamed x4, local copies, waits for them, and re-layouts  3.8 us
  transfers between devices with their start and end apart: 2, of which 0 were waited for; matrix products, arithmetic and copies ran while one was open for 1% of the time, Pallas kernels for 0%

profile of v1, /device:TPU:0, one launch (start us, length us, event | category | flops | bytes accessed | tf_op | source)
XLA Modules:
  0.0 55.9 jit_solution(3134570156179402194)
XLA Ops:
  0.6 16.2 %attend_project.1.after = bf16[64,64,128]{2,1,0:T(8,128)(2,1)} custom-call(s32[2,64]{1,0:T(2,128)} %lengths.3, s32[3,1,64]{2,1,0:T(1,128)} %bitcast.18, bf16[64,1024]{1,0:T(8,128)(2,1)} %bitcast.16, bf16[24576,128]{1,0:T(8,128)(2,1)} %bitcast.10, bf16[24576,128]{1,0:T(8,128)(2,1)} %bitcast.12, bf16[1024,8192]{1,0:T(8,128)(2,1)} %bitcast.14), custom_call_target="tpu_custom_call" | custom-call | flops 1174405120 | bytes 29360128 | tf_op jit(solution)/shard_map/attend_project/pallas_call | solution.py:119
  16.9 0.0 copy-start
  16.9 4.5 %outgoing.1 = (bf16[6144,128]{1,0:T(8,128)(2,1)}, bf16[6144,128]{1,0:T(8,128)(2,1)}) custom-call(s32[2,64]{1,0:T(2,128)} %lengths.3, s32[3,1,64]{2,1,0:T(1,128)} %bitcast.19, s32[3,16]{1,0:T(4,128)} %bitcast.20, s32[3,16]{1,0:T(4,128)} %bitcast.21, bf16[64,64,128]{2,1,0:T(8,128)(2,1)} %attend_project.1.after, bf16[24576,128]{1,0:T(8,128)(2,1)} %bitcast.11, ...), custom_call_target="tpu_custom_call" | custom-call | flops 1000000 | bytes 4718592 | tf_op jit(solution)/shard_map/outgoing/pallas_call | solution.py:180
  21.3 0.1 collective-permute-start
  21.4 0.5 collective-permute-start.1
  21.9 0.0 copy-done
  21.9 29.4 %all_to_all.5 = bf16[64,64,128]{2,1,0:T(8,128)(2,1)S(1)} all-to-all(bf16[64,64,128]{2,1,0:T(8,128)(2,1)S(1)} %copy-done), channel_id=1, replica_groups=mesh['inst'=2,'pipe'=8,'tensor'=8] {'pipe','tensor'}, dimensions={0} | all-to-all | bytes 2097152 | tf_op jit(solution)/shard_map/all_to_all | solution.py:207
  51.3 0.8 %reduce_sum.12 = bf16[64,128]{1,0:T(8,128)(2,1)} reduce(bf16[64,64,128]{2,1,0:T(8,128)(2,1)S(1)} %all_to_all.5, bf16[]{:T(256)} %constant.2.clone.1), dimensions={0}, to_apply=%region_0.0 | reduce | flops 516096 | bytes 1064962 | tf_op jit(solution)/shard_map/reduce_sum | solution.py:210
  52.1 0.0 collective-permute-done
  52.1 0.0 collective-permute-done.1
  52.1 1.1 %copy.13 = bf16[1,1,1,6144,128]{4,3,2,1,0:T(8,128)(2,1)} copy(bf16[1,1,1,6144,128]{4,3,2,1,0:T(8,128)(2,1)S(1)} %bitcast.15) | data formatting | bytes 3145728
  53.3 2.7 %copy.14 = bf16[1,1,1,6144,128]{4,3,2,1,0:T(8,128)(2,1)} copy(bf16[1,1,1,6144,128]{4,3,2,1,0:T(8,128)(2,1)} %bitcast.9) | data formatting | bytes 3145728
Async XLA Ops:
  16.9 5.1 %copy-start = (bf16[64,64,128]{2,1,0:T(8,128)(2,1)S(1)}, bf16[64,64,128]{2,1,0:T(8,128)(2,1)}, u32[]{:S(2)}) copy-start(bf16[64,64,128]{2,1,0:T(8,128)(2,1)} %attend_project.1.after) | copy-start | bytes 3145732
  21.3 30.8 %collective-permute-start = (bf16[6144,128]{1,0:T(8,128)(2,1)}, bf16[6144,128]{1,0:T(8,128)(2,1)S(1)}, u32[]{:S(2)}, u32[]{:S(2)}) collective-permute-start(bf16[6144,128]{1,0:T(8,128)(2,1)} %get-tuple-element.5), channel_id=1, source_target_pairs={{0,64},{64,0},{1,65},{65,1},{2,66},{66,2},{3,67},{67,3},{4,68},{68... | collective-permute-start | bytes 4718600 | tf_op jit(solution)/shard_map/ppermute | solution.py:209
  21.4 30.7 %collective-permute-start.1 = (bf16[6144,128]{1,0:T(8,128)(2,1)}, bf16[6144,128]{1,0:T(8,128)(2,1)}, u32[]{:S(2)}, u32[]{:S(2)}) collective-permute-start(bf16[6144,128]{1,0:T(8,128)(2,1)} %get-tuple-element.6), channel_id=1, source_target_pairs={{0,64},{64,0},{1,65},{65,1},{2,66},{66,2},{3,67},{67,3},{4,68},{68... | collective-permute-start | bytes 4718600 | tf_op jit(solution)/shard_map/ppermute | solution.py:209

commit v2 on v1

v2 whole, which is shorter than its diff:
```python
import functools
import math

import jax
import jax.numpy as jnp
from jax import lax
from jax.experimental import pallas as pl
from jax.experimental.pallas import tpu as pltpu
from jax.sharding import PartitionSpec as P


PAGE = 128
GROUP = 16
CHUNK = 512
LEAD = (3, 0, 0, 4, 4)

ATTEND_VMEM = 40
PACK_VMEM = 16

HBM = pl.BlockSpec(memory_space=pltpu.HBM)
SMEM = pl.BlockSpec(memory_space=pltpu.SMEM)
VMEM = pl.BlockSpec(memory_space=pltpu.VMEM)


def attend_kernel(
    pages,
    lengths_in, table_in, queries_in, keys, values, weight,
    out,
    lengths, page_table, queries, masked, kbuf, vbuf, wbuf, attended, staged,
    isem, qsem, ksem, vsem, wsem, osem,
):
    inst = lax.axis_index("inst")
    rows, width = queries.shape
    head_dim = keys.shape[1]
    heads = width // head_dim
    blocks = rows // GROUP
    chunks = wbuf.shape[0]
    stack = heads * GROUP
    scale = 1.0 / math.sqrt(head_dim)

    def fetch(cache, buffer, sem, block, held):
        for p in range(held):
            for g in range(GROUP):
                start = pl.multiple_of(page_table[p, 0, block * GROUP + g] * PAGE, PAGE)
                at = (block, pl.ds(p * PAGE, PAGE), pl.ds(g * head_dim, head_dim))
                pltpu.make_async_copy(
                    cache.at[pl.ds(start, PAGE)], buffer.at[at], sem.at[block]
                ).start()

    def weight_copy(chunk):
        at = pl.ds(pl.multiple_of(chunk * CHUNK, CHUNK), CHUNK)
        return pltpu.make_async_copy(weight.at[:, at], wbuf.at[chunk], wsem.at[chunk])

    def arrive(buffer, sem, block, held):
        at = (pl.ds(0, held * PAGE), pl.ds(0, GROUP * head_dim))
        pltpu.make_async_copy(weight.at[at], buffer.at[block, at[0]], sem.at[block]).wait()

    table_copy = pltpu.make_async_copy(table_in, page_table, isem.at[0])
    length_copy = pltpu.make_async_copy(lengths_in, lengths, isem.at[1])
    query_copy = pltpu.make_async_copy(queries_in, queries, qsem)
    table_copy.start()
    length_copy.start()
    query_copy.start()
    for j in range(LEAD[0]):
        weight_copy(j).start()
    row_in_group = lax.broadcasted_iota(jnp.int32, (stack, head_dim), 0) % GROUP
    lane_in_group = lax.broadcasted_iota(jnp.int32, (1, stack), 1) % GROUP

    def attend(held):
        token = lax.broadcasted_iota(jnp.int32, (held * PAGE, stack), 0)

        def score(block):
            q = queries[block * GROUP : (block + 1) * GROUP, :].astype(jnp.float32)
            q = jnp.concatenate(
                [q[:, h * head_dim : (h + 1) * head_dim] for h in range(heads)], axis=0
            )
            slot = block % 2
            for g in range(GROUP):
                masked[slot, :, g * head_dim : (g + 1) * head_dim] = jnp.where(
                    row_in_group == g, q, 0.0
                ).astype(masked.dtype)
            return lax.dot_general(
                kbuf[block, : held * PAGE], masked[slot], (((1,), (1,)), ((), ())),
                preferred_element_type=jnp.float32,
            )

        def finish(block, scores):
            limit = jnp.zeros((1, stack), jnp.int32)
            for g in range(GROUP):
                limit = jnp.where(lane_in_group == g, lengths[inst, block * GROUP + g], limit)
            scores = jnp.where(token < limit, scores, -1e30)
            top = jnp.max(scores, axis=0, keepdims=True)
            weights = jnp.exp((scores - top) * scale)
            share = 1.0 / jnp.sum(weights, axis=0, keepdims=True)
            share = jnp.broadcast_to(share, (head_dim, stack)).T
            weights = weights.T.astype(jnp.bfloat16)
            result = jnp.zeros((stack, head_dim), jnp.float32)
            for g in range(0, GROUP, 2):
                pair = jnp.dot(
                    weights, vbuf[block, : held * PAGE, g * head_dim : (g + 2) * head_dim],
                    preferred_element_type=jnp.float32,
                )
                result = jnp.where(row_in_group == g, pair[:, :head_dim], result)
                result = jnp.where(row_in_group == g + 1, pair[:, head_dim:], result)
            result = result * share
            for h in range(heads):
                attended[
                    block * GROUP : (block + 1) * GROUP, h * head_dim : (h + 1) * head_dim
                ] = result[h * GROUP : (h + 1) * GROUP, :].astype(attended.dtype)

        fetch(keys, kbuf, ksem, 0, held)
        fetch(values, vbuf, vsem, 0, held)
        fetch(keys, kbuf, ksem, 1, held)
        fetch(values, vbuf, vsem, 1, held)
        length_copy.wait()
        query_copy.wait()
        arrive(kbuf, ksem, 0, held)
        scores = score(0)
        for block in range(blocks):
            if block + 2 < blocks:
                fetch(keys, kbuf, ksem, block + 2, held)
                fetch(values, vbuf, vsem, block + 2, held)
            for j in range(sum(LEAD[: block + 1]), sum(LEAD[: block + 2])):
                weight_copy(j).start()
            arrive(vbuf, vsem, block, held)
            if block + 1 < blocks:
                arrive(kbuf, ksem, block + 1, held)
                following = score(block + 1)
            finish(block, scores)
            scores = following

    table_copy.wait()

    @pl.when(inst == 0)
    def _():
        attend(pages - 1)

    @pl.when(inst != 0)
    def _():
        attend(pages)

    piece = out.shape[2]
    per_chunk = CHUNK // piece

    def store(chunk):
        at = pl.ds(chunk * per_chunk, per_chunk)
        return pltpu.make_async_copy(staged.at[at], out.at[at], osem.at[chunk])

    def project(chunk, _):
        @pl.when(chunk + sum(LEAD) < chunks)
        def _():
            weight_copy(chunk + sum(LEAD)).start()

        weight_copy(chunk).wait()
        part = jnp.dot(attended[...], wbuf[chunk], preferred_element_type=jnp.float32)
        for j in range(per_chunk):
            staged[chunk * per_chunk + j] = part[:, j * piece : (j + 1) * piece].astype(
                out.dtype
            )
        store(chunk).start()
        return 0

    lax.fori_loop(0, chunks, project, 0)
    lax.fori_loop(0, chunks, lambda chunk, _: (store(chunk).wait(), 0)[1], 0)


def attend_project(lengths, page_table, queries, keys, values, weight, parts):
    rows, width = queries.shape
    head_dim = keys.shape[1]
    pages = page_table.shape[0]
    blocks = rows // GROUP
    depth, columns = weight.shape
    chunks = columns // CHUNK
    cache = pltpu.VMEM((blocks, pages * PAGE, GROUP * head_dim), keys.dtype)
    return pl.pallas_call(
        functools.partial(attend_kernel, pages),
        out_shape=jax.ShapeDtypeStruct((parts, rows, columns // parts), jnp.bfloat16),
        in_specs=[HBM] * 6,
        out_specs=HBM,
        scratch_shapes=[
            pltpu.SMEM(lengths.shape, jnp.int32),
            pltpu.SMEM(page_table.shape, jnp.int32),
            pltpu.VMEM(queries.shape, queries.dtype),
            pltpu.VMEM((2, width // head_dim * GROUP, GROUP * head_dim), queries.dtype),
            cache,
            cache,
            pltpu.VMEM((chunks, depth, CHUNK), weight.dtype),
            pltpu.VMEM((rows, width), jnp.bfloat16),
            pltpu.VMEM((parts, rows, columns // parts), jnp.bfloat16),
            pltpu.SemaphoreType.DMA((2,)),
            pltpu.SemaphoreType.DMA,
            pltpu.SemaphoreType.DMA((blocks,)),
            pltpu.SemaphoreType.DMA((blocks,)),
            pltpu.SemaphoreType.DMA((chunks,)),
            pltpu.SemaphoreType.DMA((chunks,)),
        ],
        compiler_params=pltpu.CompilerParams(vmem_limit_bytes=ATTEND_VMEM * 1024 * 1024),
        cost_estimate=pl.CostEstimate(
            flops=2 * rows * depth * columns + 4 * rows * width * pages * PAGE,
            bytes_accessed=2 * (weight.size + 2 * keys.size),
            transcendentals=0,
        ),
        name="attend_project",
    )(lengths, page_table, queries, keys, values, weight)


def pack_kernel(page_table, migration, keys, values, packed, sem):
    moves = migration.shape[1] // 2
    pages = page_table.shape[0]
    first = (1 - lax.axis_index("inst")) * moves
    half = packed.shape[0] // 2
    for k in range(moves):
        request = migration[0, first + k]
        for p in range(pages):
            source = pl.ds(pl.multiple_of(page_table[p, 0, request] * PAGE, PAGE), PAGE)
            at = (k * pages + p) * PAGE
            pltpu.make_async_copy(keys.at[source], packed.at[pl.ds(at, PAGE)], sem).start()
            pltpu.make_async_copy(
                values.at[source], packed.at[pl.ds(half + at, PAGE)], sem
            ).start()
    pltpu.make_async_copy(keys.at[pl.ds(0, 2 * half)], packed, sem).wait()


def pack(page_table, migration, keys, values):
    slots = migration.shape[1] // 2 * page_table.shape[0]
    packed = jax.ShapeDtypeStruct((2 * slots * PAGE, keys.shape[1]), keys.dtype)
    return pl.pallas_call(
        pack_kernel,
        out_shape=pltpu.VMEM(packed.shape, packed.dtype),
        in_specs=[SMEM, SMEM, HBM, HBM],
        out_specs=VMEM,
        scratch_shapes=[pltpu.SemaphoreType.DMA],
        compiler_params=pltpu.CompilerParams(vmem_limit_bytes=PACK_VMEM * 1024 * 1024),
        cost_estimate=pl.CostEstimate(
            flops=1_000_000, bytes_accessed=4 * packed.size, transcendentals=0
        ),
        name="pack",
    )(page_table, migration, keys, values)


def place_kernel(lengths, migration, dest_slots, packed, key_area, value_area, blank, ksem, vsem):
    inst = lax.axis_index("inst")
    pages, moves = dest_slots.shape
    half = packed.shape[0] // 2
    blank[...] = jnp.zeros_like(blank)
    for m in range(moves):
        from_inst = 1 if m < moves // 2 else 0
        held = lengths[from_inst, migration[0, m]]
        for p in range(pages):
            target = pl.ds(pl.multiple_of(dest_slots[p, m] * PAGE, PAGE), PAGE)
            at = (m % (moves // 2) * pages + p) * PAGE
            live = (inst != from_inst) & (p * PAGE < held)
            for area, sem, offset in ((key_area, ksem, at), (value_area, vsem, half + at)):

                @pl.when(live)
                def _():
                    pltpu.make_async_copy(
                        packed.at[pl.ds(offset, PAGE)], area.at[target], sem
                    ).start()

                @pl.when(jnp.logical_not(live))
                def _():
                    pltpu.make_async_copy(blank, area.at[target], sem).start()

    for area, sem in ((key_area, ksem), (value_area, vsem)):
        pltpu.make_async_copy(area, area, sem).wait()


def place(lengths, migration, dest_slots, packed):
    area = jax.ShapeDtypeStruct((dest_slots.size * PAGE, packed.shape[1]), packed.dtype)
    return pl.pallas_call(
        place_kernel,
        out_shape=(area, area),
        in_specs=[SMEM, SMEM, SMEM, VMEM],
        out_specs=(HBM, HBM),
        scratch_shapes=[
            pltpu.VMEM((PAGE, packed.shape[1]), packed.dtype),
            pltpu.SemaphoreType.DMA,
            pltpu.SemaphoreType.DMA,
        ],
        compiler_params=pltpu.CompilerParams(vmem_limit_bytes=PACK_VMEM * 1024 * 1024),
        cost_estimate=pl.CostEstimate(
            flops=1_000_000, bytes_accessed=4 * area.size, transcendentals=0
        ),
        name="place",
    )(lengths, migration, dest_slots, packed)


def body(lengths, page_table, migration, dest_slots, queries, key_cache, value_cache, out_weight):
    parts = lax.axis_size("pipe") * lax.axis_size("tensor")
    (lengths, page_table, migration, dest_slots, queries, keys, values, weight) = [
        pltpu.with_memory_space_constraint(array, pltpu.HBM)
        for array in (
            lengths,
            jnp.transpose(page_table, (2, 0, 1)),
            migration.T,
            dest_slots.T,
            queries.reshape(queries.shape[2:]),
            key_cache.reshape(key_cache.shape[3:]),
            value_cache.reshape(value_cache.shape[3:]),
            out_weight.reshape(out_weight.shape[1:]),
        )
    ]
    partial = attend_project(lengths, page_table, queries, keys, values, weight, parts)
    arrived = lax.all_to_all(partial, ("pipe", "tensor"), split_axis=0, concat_axis=0, tiled=True)
    packed = pack(page_table, migration, keys, values)
    moved = lax.ppermute(packed, "inst", [(0, 1), (1, 0)])
    received = place(lengths, migration, dest_slots, moved)
    update = arrived.astype(jnp.float32).sum(axis=0).astype(jnp.bfloat16)
    return (update[None], *[r.reshape(1, 1, 1, *r.shape) for r in received])


def solution(mesh):
    placed = (
        P(),
        P("inst", None, None),
        P(),
        P(),
        P("inst", "pipe", None, "tensor"),
        P("inst", "pipe", "tensor", None, None),
        P("inst", "pipe", "tensor", None, None),
        P("pipe", "tensor", None),
    )
    return jax.shard_map(
        body,
        mesh=mesh,
        in_specs=placed,
        out_specs=(
            P("inst", None, ("pipe", "tensor")),
            P("inst", "pipe", "tensor", None, None),
            P("inst", "pipe", "tensor", None, None),
        ),
        check_vma=False,
    )
```

time: 56.2 us -> 52.3 us (0.931)
  the two profiles are of different devices: /device:TPU:0 before, /device:TPU:1 now
where the time goes in v2:
time: 52.3 us; the launch traced here: 51.9 us
  blocking collectives  28.2 us (54%)
  Pallas kernels  19.6 us (37%)
  other arithmetic  2.01 us (4%)
  starting transfers between devices  1.45 us (3%)
  between operations  0.65 us (1%)
    all_to_all x1, blocking collectives, body(): lax.all_to_all(partial, ('pipe', 'tensor'), split_axis=0, concat_axis=0,...  28.2 us
    pallas_call x1, Pallas kernels, attend_project(): pl.pallas_call(functools.partial(attend_kernel, pages), out_shape=jax.Sha...  15.1 us
    pallas_call x1, Pallas kernels, place(): pl.pallas_call(place_kernel, out_shape=(area, area), in_specs=[SMEM, SMEM...  2.38 us
    pallas_call x1, Pallas kernels, pack(): pl.pallas_call(pack_kernel, out_shape=pltpu.VMEM(packed.shape, packed.dty...  2.08 us
    reduce_sum x1, other arithmetic, body(): update = arrived.astype(jnp.float32).sum(axis=0).astype(jnp.bfloat16)  2.01 us
    ppermute x1, starting transfers between devices, body(): moved = lax.ppermute(packed, 'inst', [(0, 1), (1, 0)])  1.45 us
  transfers between devices with their start and end apart: 1, of which 0 were waited for; matrix products, arithmetic and copies ran while one was open for 4% of the time, Pallas kernels for 29%

profile of v2, /device:TPU:1, one launch (start us, length us, event | category | flops | bytes accessed | tf_op | source)
XLA Modules:
  0.0 51.9 jit_solution(1605384874798722986)
XLA Ops:
  0.6 2.1 %pack.1 = bf16[6144,128]{1,0:T(8,128)(2,1)S(1)} custom-call(s32[3,1,64]{2,1,0:T(1,128)} %bitcast.19, s32[3,16]{1,0:T(4,128)} %bitcast.17, bf16[24576,128]{1,0:T(8,128)(2,1)} %bitcast.10, bf16[24576,128]{1,0:T(8,128)(2,1)} %bitcast.12), custom_call_target="tpu_custom_call" | custom-call | flops 1000000 | bytes 3145728 | tf_op jit(solution)/shard_map/pack/pallas_call | solution.py:227
  2.7 1.5 %collective-permute-start = (bf16[6144,128]{1,0:T(8,128)(2,1)S(1)}, bf16[6144,128]{1,0:T(8,128)(2,1)S(1)}, u32[]{:S(2)}, u32[]{:S(2)}) collective-permute-start(bf16[6144,128]{1,0:T(8,128)(2,1)S(1)} %pack.1), channel_id=1, source_target_pairs={{0,64},{64,0},{1,65},{65,1},{2,66},{66,2},{3,67},{67,3},{4,68},{68... | collective-permute-start | bytes 4718600 | tf_op jit(solution)/shard_map/ppermute | solution.py:307
  4.2 15.1 %attend_project.1 = bf16[64,64,128]{2,1,0:T(8,128)(2,1)S(1)} custom-call(s32[2,64]{1,0:T(2,128)} %lengths.1, s32[3,1,64]{2,1,0:T(1,128)} %bitcast.20, bf16[64,1024]{1,0:T(8,128)(2,1)} %bitcast.15, bf16[24576,128]{1,0:T(8,128)(2,1)} %bitcast.11, bf16[24576,128]{1,0:T(8,128)(2,1)} %bitcast.13, bf16[1024,8192]{1,0:T(8,128)(2,1)} %bitcast.14), custom_call_target="tpu_custom_call" | custom-call | flops 1174405120 | bytes 29360128 | tf_op jit(solution)/shard_map/attend_project/pallas_call | solution.py:175
  19.3 28.2 %all_to_all.5 = bf16[64,64,128]{2,1,0:T(8,128)(2,1)} all-to-all(bf16[64,64,128]{2,1,0:T(8,128)(2,1)S(1)} %attend_project.1), channel_id=1, replica_groups=mesh['inst'=2,'pipe'=8,'tensor'=8] {'pipe','tensor'}, dimensions={0} | all-to-all | bytes 2097152 | tf_op jit(solution)/shard_map/all_to_all | solution.py:305
  47.5 2.0 %reduce_sum.12 = bf16[64,128]{1,0:T(8,128)(2,1)} reduce(bf16[64,64,128]{2,1,0:T(8,128)(2,1)} %all_to_all.5, bf16[]{:T(256)} %constant.2.clone.1), dimensions={0}, to_apply=%region_0.0 | reduce | flops 516096 | bytes 1064962 | tf_op jit(solution)/shard_map/reduce_sum | solution.py:309
  49.5 0.0 collective-permute-done.packed
  49.5 2.4 %place.1 = (bf16[6144,128]{1,0:T(8,128)(2,1)}, bf16[6144,128]{1,0:T(8,128)(2,1)}) custom-call(s32[2,64]{1,0:T(2,128)} %lengths.1, s32[3,16]{1,0:T(4,128)} %bitcast.18, s32[3,16]{1,0:T(4,128)} %bitcast.21, bf16[6144,128]{1,0:T(8,128)(2,1)S(1)} %collective-permute-done.packed), custom_call_target="tpu_custom_call" | custom-call | flops 1000000 | bytes 3145728 | tf_op jit(solution)/shard_map/place/pallas_call | solution.py:271
Async XLA Ops:
  2.7 46.8 %collective-permute-start = (bf16[6144,128]{1,0:T(8,128)(2,1)S(1)}, bf16[6144,128]{1,0:T(8,128)(2,1)S(1)}, u32[]{:S(2)}, u32[]{:S(2)}) collective-permute-start(bf16[6144,128]{1,0:T(8,128)(2,1)S(1)} %pack.1), channel_id=1, source_target_pairs={{0,64},{64,0},{1,65},{65,1},{2,66},{66,2},{3,67},{67,3},{4,68},{68... | collective-permute-start | bytes 4718600 | tf_op jit(solution)/shard_map/ppermute | solution.py:307

commit v3 on v2

--- a/solution.py
+++ b/solution.py
@@ -11,8 +11,9 @@
 
 PAGE = 128
 GROUP = 16
-CHUNK = 512
-LEAD = (3, 0, 0, 4, 4)
+CHUNK = 1024
+LEAD = (0, 0, 1, 2, 2)
+KEY_COPIES = 8
 
 ATTEND_VMEM = 40
 PACK_VMEM = 16
@@ -26,7 +27,7 @@
     pages,
     lengths_in, table_in, queries_in, keys, values, weight,
     out,
-    lengths, page_table, queries, masked, kbuf, vbuf, wbuf, attended, staged,
+    lengths, page_table, queries, kbuf, vbuf, wbuf, attended, staged,
     isem, qsem, ksem, vsem, wsem, osem,
 ):
     inst = lax.axis_index("inst")
@@ -38,22 +39,28 @@
     stack = heads * GROUP
     scale = 1.0 / math.sqrt(head_dim)
 
-    def fetch(cache, buffer, sem, block, held):
+    def page(p, request):
+        return pl.ds(pl.multiple_of(page_table[p, 0, request] * PAGE, PAGE), PAGE)
+
+    def fetch_values(block, held):
         for p in range(held):
             for g in range(GROUP):
-                start = pl.multiple_of(page_table[p, 0, block * GROUP + g] * PAGE, PAGE)
                 at = (block, pl.ds(p * PAGE, PAGE), pl.ds(g * head_dim, head_dim))
                 pltpu.make_async_copy(
-                    cache.at[pl.ds(start, PAGE)], buffer.at[at], sem.at[block]
+                    values.at[page(p, block * GROUP + g)], vbuf.at[at], vsem.at[block]
                 ).start()
 
     def weight_copy(chunk):
         at = pl.ds(pl.multiple_of(chunk * CHUNK, CHUNK), CHUNK)
         return pltpu.make_async_copy(weight.at[:, at], wbuf.at[chunk], wsem.at[chunk])
 
-    def arrive(buffer, sem, block, held):
+    def values_arrive(block, held):
         at = (pl.ds(0, held * PAGE), pl.ds(0, GROUP * head_dim))
-        pltpu.make_async_copy(weight.at[at], buffer.at[block, at[0]], sem.at[block]).wait()
+        pltpu.make_async_copy(weight.at[at], vbuf.at[block, at[0]], vsem.at[block]).wait()
+
+    def key_copy(part):
+        at = pl.ds(part * (keys.shape[0] // KEY_COPIES), keys.shape[0] // KEY_COPIES)
+        return pltpu.make_async_copy(keys.at[at], kbuf.at[at], ksem.at[part])
 
     table_copy = pltpu.make_async_copy(table_in, page_table, isem.at[0])
     length_copy = pltpu.make_async_copy(lengths_in, lengths, isem.at[1])
@@ -61,6 +68,8 @@
     table_copy.start()
     length_copy.start()
     query_copy.start()
+    for part in range(KEY_COPIES):
+        key_copy(part).start()
     for j in range(LEAD[0]):
         weight_copy(j).start()
     row_in_group = lax.broadcasted_iota(jnp.int32, (stack, head_dim), 0) % GROUP
@@ -74,15 +83,25 @@
             q = jnp.concatenate(
                 [q[:, h * head_dim : (h + 1) * head_dim] for h in range(heads)], axis=0
             )
-            slot = block % 2
-            for g in range(GROUP):
-                masked[slot, :, g * head_dim : (g + 1) * head_dim] = jnp.where(
-                    row_in_group == g, q, 0.0
-                ).astype(masked.dtype)
-            return lax.dot_general(
-                kbuf[block, : held * PAGE], masked[slot], (((1,), (1,)), ((), ())),
-                preferred_element_type=jnp.float32,
-            )
+            total = None
+            for g in range(0, GROUP, 2):
+                pair = jnp.concatenate(
+                    [jnp.where(row_in_group == g + e, q, 0.0) for e in range(2)], axis=1
+                ).astype(jnp.bfloat16)
+                k = jnp.concatenate(
+                    [
+                        jnp.concatenate(
+                            [kbuf[page(p, block * GROUP + g + e), :] for e in range(2)], axis=1
+                        )
+                        for p in range(held)
+                    ],
+                    axis=0,
+                )
+                part = lax.dot_general(
+                    k, pair, (((1,), (1,)), ((), ())), preferred_element_type=jnp.float32
+                )
+                total = part if total is None else total + part
+            return total
 
         def finish(block, scores):
             limit = jnp.zeros((1, stack), jnp.int32)
@@ -108,23 +127,20 @@
                     block * GROUP : (block + 1) * GROUP, h * head_dim : (h + 1) * head_dim
                 ] = result[h * GROUP : (h + 1) * GROUP, :].astype(attended.dtype)
 
-        fetch(keys, kbuf, ksem, 0, held)
-        fetch(values, vbuf, vsem, 0, held)
-        fetch(keys, kbuf, ksem, 1, held)
-        fetch(values, vbuf, vsem, 1, held)
+        fetch_values(0, held)
+        fetch_values(1, held)
         length_copy.wait()
         query_copy.wait()
-        arrive(kbuf, ksem, 0, held)
+        for part in range(KEY_COPIES):
+            key_copy(part).wait()
         scores = score(0)
         for block in range(blocks):
             if block + 2 < blocks:
-                fetch(keys, kbuf, ksem, block + 2, held)
-                fetch(values, vbuf, vsem, block + 2, held)
+                fetch_values(block + 2, held)
             for j in range(sum(LEAD[: block + 1]), sum(LEAD[: block + 2])):
                 weight_copy(j).start()
-            arrive(vbuf, vsem, block, held)
+            values_arrive(block, held)
             if block + 1 < blocks:
-                arrive(kbuf, ksem, block + 1, held)
                 following = score(block + 1)
             finish(block, scores)
             scores = following
@@ -171,7 +187,6 @@
     blocks = rows // GROUP
     depth, columns = weight.shape
     chunks = columns // CHUNK
-    cache = pltpu.VMEM((blocks, pages * PAGE, GROUP * head_dim), keys.dtype)
     return pl.pallas_call(
         functools.partial(attend_kernel, pages),
         out_shape=jax.ShapeDtypeStruct((parts, rows, columns // parts), jnp.bfloat16),
@@ -181,15 +196,14 @@
             pltpu.SMEM(lengths.shape, jnp.int32),
             pltpu.SMEM(page_table.shape, jnp.int32),
             pltpu.VMEM(queries.shape, queries.dtype),
-            pltpu.VMEM((2, width // head_dim * GROUP, GROUP * head_dim), queries.dtype),
-            cache,
-            cache,
+            pltpu.VMEM(keys.shape, keys.dtype),
+            pltpu.VMEM((blocks, pages * PAGE, GROUP * head_dim), values.dtype),
             pltpu.VMEM((chunks, depth, CHUNK), weight.dtype),
             pltpu.VMEM((rows, width), jnp.bfloat16),
             pltpu.VMEM((parts, rows, columns // parts), jnp.bfloat16),
             pltpu.SemaphoreType.DMA((2,)),
             pltpu.SemaphoreType.DMA,
-            pltpu.SemaphoreType.DMA((blocks,)),
+            pltpu.SemaphoreType.DMA((KEY_COPIES,)),
             pltpu.SemaphoreType.DMA((blocks,)),
             pltpu.SemaphoreType.DMA((chunks,)),
             pltpu.SemaphoreType.DMA((chunks,)),

time: 52.3 us -> 50.5 us (0.966)
  Pallas kernels: 19.6 us -> 17.6 us
    pallas_call x1, Pallas kernels: 15.1 us -> 13.1 us  [attend_project(): pl.pallas_call(functools.partial(attend_kernel, pages), out_shape=jax.Sha...]
  transfers between devices with their start and end apart: 1 -> 1, of which waited for: 0 -> 0; matrix products, arithmetic and copies ran while one was open for 4% -> 4% of each run, Pallas kernels for 29% -> 26%
where the time goes in v3:
time: 50.5 us; the launch traced here: 50.2 us
  blocking collectives  28.5 us (56%)
  Pallas kernels  17.6 us (35%)
  other arithmetic  2.01 us (4%)
  starting transfers between devices  1.45 us (3%)
  between operations  0.65 us (1%)
    all_to_all x1, blocking collectives, body(): lax.all_to_all(partial, ('pipe', 'tensor'), split_axis=0, concat_axis=0,...  28.5 us
    pallas_call x1, Pallas kernels, attend_project(): pl.pallas_call(functools.partial(attend_kernel, pages), out_shape=jax.Sha...  13.1 us
    pallas_call x1, Pallas kernels, place(): pl.pallas_call(place_kernel, out_shape=(area, area), in_specs=[SMEM, SMEM...  2.38 us
    pallas_call x1, Pallas kernels, pack(): pl.pallas_call(pack_kernel, out_shape=pltpu.VMEM(packed.shape, packed.dty...  2.08 us
    reduce_sum x1, other arithmetic, body(): update = arrived.astype(jnp.float32).sum(axis=0).astype(jnp.bfloat16)  2.01 us
    ppermute x1, starting transfers between devices, body(): moved = lax.ppermute(packed, 'inst', [(0, 1), (1, 0)])  1.45 us
  transfers between devices with their start and end apart: 1, of which 0 were waited for; matrix products, arithmetic and copies ran while one was open for 4% of the time, Pallas kernels for 26%

profile of v3, /device:TPU:1, one launch (start us, length us, event | category | flops | bytes accessed | tf_op | source)
XLA Modules:
  0.0 50.2 jit_solution(11050638966307961183)
XLA Ops:
  0.6 2.1 %pack.1 = bf16[6144,128]{1,0:T(8,128)(2,1)S(1)} custom-call(s32[3,1,64]{2,1,0:T(1,128)} %bitcast.19, s32[3,16]{1,0:T(4,128)} %bitcast.17, bf16[24576,128]{1,0:T(8,128)(2,1)} %bitcast.10, bf16[24576,128]{1,0:T(8,128)(2,1)} %bitcast.12), custom_call_target="tpu_custom_call" | custom-call | flops 1000000 | bytes 3145728 | tf_op jit(solution)/shard_map/pack/pallas_call | solution.py:241
  2.7 1.5 %collective-permute-start = (bf16[6144,128]{1,0:T(8,128)(2,1)S(1)}, bf16[6144,128]{1,0:T(8,128)(2,1)S(1)}, u32[]{:S(2)}, u32[]{:S(2)}) collective-permute-start(bf16[6144,128]{1,0:T(8,128)(2,1)S(1)} %pack.1), channel_id=1, source_target_pairs={{0,64},{64,0},{1,65},{65,1},{2,66},{66,2},{3,67},{67,3},{4,68},{68... | collective-permute-start | bytes 4718600 | tf_op jit(solution)/shard_map/ppermute | solution.py:321
  4.2 13.1 %attend_project.1 = bf16[64,64,128]{2,1,0:T(8,128)(2,1)S(1)} custom-call(s32[2,64]{1,0:T(2,128)} %lengths.1, s32[3,1,64]{2,1,0:T(1,128)} %bitcast.20, bf16[64,1024]{1,0:T(8,128)(2,1)} %bitcast.15, bf16[24576,128]{1,0:T(8,128)(2,1)} %bitcast.11, bf16[24576,128]{1,0:T(8,128)(2,1)} %bitcast.13, bf16[1024,8192]{1,0:T(8,128)(2,1)} %bitcast.14), custom_call_target="tpu_custom_call" | custom-call | flops 1174405120 | bytes 29360128 | tf_op jit(solution)/shard_map/attend_project/pallas_call | solution.py:190
  17.3 28.5 %all_to_all.5 = bf16[64,64,128]{2,1,0:T(8,128)(2,1)} all-to-all(bf16[64,64,128]{2,1,0:T(8,128)(2,1)S(1)} %attend_project.1), channel_id=1, replica_groups=mesh['inst'=2,'pipe'=8,'tensor'=8] {'pipe','tensor'}, dimensions={0} | all-to-all | bytes 2097152 | tf_op jit(solution)/shard_map/all_to_all | solution.py:319
  45.8 2.0 %reduce_sum.12 = bf16[64,128]{1,0:T(8,128)(2,1)} reduce(bf16[64,64,128]{2,1,0:T(8,128)(2,1)} %all_to_all.5, bf16[]{:T(256)} %constant.2.clone.1), dimensions={0}, to_apply=%region_0.0 | reduce | flops 516096 | bytes 1064962 | tf_op jit(solution)/shard_map/reduce_sum | solution.py:323
  47.8 0.0 collective-permute-done.packed
  47.8 2.4 %place.1 = (bf16[6144,128]{1,0:T(8,128)(2,1)}, bf16[6144,128]{1,0:T(8,128)(2,1)}) custom-call(s32[2,64]{1,0:T(2,128)} %lengths.1, s32[3,16]{1,0:T(4,128)} %bitcast.18, s32[3,16]{1,0:T(4,128)} %bitcast.21, bf16[6144,128]{1,0:T(8,128)(2,1)S(1)} %collective-permute-done.packed), custom_call_target="tpu_custom_call" | custom-call | flops 1000000 | bytes 3145728 | tf_op jit(solution)/shard_map/place/pallas_call | solution.py:285
Async XLA Ops:
  2.7 45.1 %collective-permute-start = (bf16[6144,128]{1,0:T(8,128)(2,1)S(1)}, bf16[6144,128]{1,0:T(8,128)(2,1)S(1)}, u32[]{:S(2)}, u32[]{:S(2)}) collective-permute-start(bf16[6144,128]{1,0:T(8,128)(2,1)S(1)} %pack.1), channel_id=1, source_target_pairs={{0,64},{64,0},{1,65},{65,1},{2,66},{66,2},{3,67},{67,3},{4,68},{68... | collective-permute-start | bytes 4718600 | tf_op jit(solution)/shard_map/ppermute | solution.py:321

commit v4 on v3

--- a/solution.py
+++ b/solution.py
@@ -162,11 +162,9 @@
         at = pl.ds(chunk * per_chunk, per_chunk)
         return pltpu.make_async_copy(staged.at[at], out.at[at], osem.at[chunk])
 
-    def project(chunk, _):
-        @pl.when(chunk + sum(LEAD) < chunks)
-        def _():
+    def project(chunk):
+        if chunk + sum(LEAD) < chunks:
             weight_copy(chunk + sum(LEAD)).start()
-
         weight_copy(chunk).wait()
         part = jnp.dot(attended[...], wbuf[chunk], preferred_element_type=jnp.float32)
         for j in range(per_chunk):
@@ -174,9 +172,9 @@
                 out.dtype
             )
         store(chunk).start()
-        return 0
-
-    lax.fori_loop(0, chunks, project, 0)
+
+    for chunk in range(chunks):
+        project(chunk)
     lax.fori_loop(0, chunks, lambda chunk, _: (store(chunk).wait(), 0)[1], 0)
 
 

time: 50.5 us -> 50.5 us (level)
  no operation moved by 1% of the time
where the time goes in v4:
time: 50.5 us; the launch traced here: 50.1 us
  blocking collectives  28.5 us (56%)
  Pallas kernels  17.5 us (35%)
  other arithmetic  2.01 us (4%)
  starting transfers between devices  1.45 us (3%)
  between operations  0.65 us (1%)
    all_to_all x1, blocking collectives, body(): lax.all_to_all(partial, ('pipe', 'tensor'), split_axis=0, concat_axis=0,...  28.5 us
    pallas_call x1, Pallas kernels, attend_project(): pl.pallas_call(functools.partial(attend_kernel, pages), out_shape=jax.Sha...  13 us
    pallas_call x1, Pallas kernels, place(): pl.pallas_call(place_kernel, out_shape=(area, area), in_specs=[SMEM, SMEM...  2.38 us
    pallas_call x1, Pallas kernels, pack(): pl.pallas_call(pack_kernel, out_shape=pltpu.VMEM(packed.shape, packed.dty...  2.08 us
    reduce_sum x1, other arithmetic, body(): update = arrived.astype(jnp.float32).sum(axis=0).astype(jnp.bfloat16)  2.01 us
    ppermute x1, starting transfers between devices, body(): moved = lax.ppermute(packed, 'inst', [(0, 1), (1, 0)])  1.45 us
  transfers between devices with their start and end apart: 1, of which 0 were waited for; matrix products, arithmetic and copies ran while one was open for 4% of the time, Pallas kernels for 26%

profile of v4, /device:TPU:1, one launch (start us, length us, event | category | flops | bytes accessed | tf_op | source)
XLA Modules:
  0.0 50.1 jit_solution(14474572260428799321)
XLA Ops:
  0.6 2.1 %pack.1 = bf16[6144,128]{1,0:T(8,128)(2,1)S(1)} custom-call(s32[3,1,64]{2,1,0:T(1,128)} %bitcast.19, s32[3,16]{1,0:T(4,128)} %bitcast.17, bf16[24576,128]{1,0:T(8,128)(2,1)} %bitcast.10, bf16[24576,128]{1,0:T(8,128)(2,1)} %bitcast.12), custom_call_target="tpu_custom_call" | custom-call | flops 1000000 | bytes 3145728 | tf_op jit(solution)/shard_map/pack/pallas_call | solution.py:239
  2.7 1.5 %collective-permute-start = (bf16[6144,128]{1,0:T(8,128)(2,1)S(1)}, bf16[6144,128]{1,0:T(8,128)(2,1)S(1)}, u32[]{:S(2)}, u32[]{:S(2)}) collective-permute-start(bf16[6144,128]{1,0:T(8,128)(2,1)S(1)} %pack.1), channel_id=1, source_target_pairs={{0,64},{64,0},{1,65},{65,1},{2,66},{66,2},{3,67},{67,3},{4,68},{68... | collective-permute-start | bytes 4718600 | tf_op jit(solution)/shard_map/ppermute | solution.py:319
  4.2 13.0 %attend_project.1 = bf16[64,64,128]{2,1,0:T(8,128)(2,1)S(1)} custom-call(s32[2,64]{1,0:T(2,128)} %lengths.1, s32[3,1,64]{2,1,0:T(1,128)} %bitcast.20, bf16[64,1024]{1,0:T(8,128)(2,1)} %bitcast.15, bf16[24576,128]{1,0:T(8,128)(2,1)} %bitcast.11, bf16[24576,128]{1,0:T(8,128)(2,1)} %bitcast.13, bf16[1024,8192]{1,0:T(8,128)(2,1)} %bitcast.14), custom_call_target="tpu_custom_call" | custom-call | flops 1174405120 | bytes 29360128 | tf_op jit(solution)/shard_map/attend_project/pallas_call | solution.py:188
  17.2 28.5 %all_to_all.5 = bf16[64,64,128]{2,1,0:T(8,128)(2,1)} all-to-all(bf16[64,64,128]{2,1,0:T(8,128)(2,1)S(1)} %attend_project.1), channel_id=1, replica_groups=mesh['inst'=2,'pipe'=8,'tensor'=8] {'pipe','tensor'}, dimensions={0} | all-to-all | bytes 2097152 | tf_op jit(solution)/shard_map/all_to_all | solution.py:317
  45.7 2.0 %reduce_sum.12 = bf16[64,128]{1,0:T(8,128)(2,1)} reduce(bf16[64,64,128]{2,1,0:T(8,128)(2,1)} %all_to_all.5, bf16[]{:T(256)} %constant.2.clone.1), dimensions={0}, to_apply=%region_0.0 | reduce | flops 516096 | bytes 1064962 | tf_op jit(solution)/shard_map/reduce_sum | solution.py:321
  47.7 0.0 collective-permute-done.packed
  47.7 2.4 %place.1 = (bf16[6144,128]{1,0:T(8,128)(2,1)}, bf16[6144,128]{1,0:T(8,128)(2,1)}) custom-call(s32[2,64]{1,0:T(2,128)} %lengths.1, s32[3,16]{1,0:T(4,128)} %bitcast.18, s32[3,16]{1,0:T(4,128)} %bitcast.21, bf16[6144,128]{1,0:T(8,128)(2,1)S(1)} %collective-permute-done.packed), custom_call_target="tpu_custom_call" | custom-call | flops 1000000 | bytes 3145728 | tf_op jit(solution)/shard_map/place/pallas_call | solution.py:283
Async XLA Ops:
  2.7 45.0 %collective-permute-start = (bf16[6144,128]{1,0:T(8,128)(2,1)S(1)}, bf16[6144,128]{1,0:T(8,128)(2,1)S(1)}, u32[]{:S(2)}, u32[]{:S(2)}) collective-permute-start(bf16[6144,128]{1,0:T(8,128)(2,1)S(1)} %pack.1), channel_id=1, source_target_pairs={{0,64},{64,0},{1,65},{65,1},{2,66},{66,2},{3,67},{67,3},{4,68},{68... | collective-permute-start | bytes 4718600 | tf_op jit(solution)/shard_map/ppermute | solution.py:319
